TPU v7x, 32 devices: a whole 2x2x4 slice. The times are simulated.
32 devices in a mesh: row: 8 (over z, x), mem: 2 (over core), lev: 2 (over y).
Axes of the slice: x: 2, y: 2, z: 4, core: 2. Of those that a mesh axis runs over, the one named last changes fastest.
Arguments:
- control_fields: bfloat16 [4, 6, 256, 2048], P('mem', 'lev', 'row'), may hold values from -6 to 6
- perturbations: bfloat16 [3, 4, 6, 256, 2048], P(None, 'mem', 'lev', 'row'), may hold values from -3 to 3
- column_taper: bfloat16 [2048, 2048], P('row'), may hold values from -1 to 2, as said below
- row_taper: bfloat16 [256, 256], P('row'), may hold values from -1 to 2, as said below
- courant_numbers: float32 [3, 6, 256, 2048], P(None, 'lev', 'row', 'mem'), may hold values from -0.3 to 0.3
- tracer_slope: float32 [2, 6, 256, 2048], P(None, 'lev', 'row', 'mem'), may hold values from -3 to 3
Outputs:
- increment: float32 [3, 6, 256, 2048], P(None, 'lev', 'row', 'mem')
Inputs may be any that keep to these rules, and one draw needn't show every extreme that they name: `column_taper`: A square matrix. `row_taper`: A square matrix.
All inputs are finite; a program needn't handle non-finite values.
Results may differ from a plain program's by a relative error of at most 0.0048.
Values may be sent and summed in bfloat16 or wider, within the bound.
A program may use at most 64 MiB of HBM per device.

v0:
```python
import jax
import jax.numpy as jnp
from jax import lax
from jax.sharding import PartitionSpec as P

STEPS = 4


def faces(block, axis, dim):
    count = lax.axis_size(axis)
    forward = [(i, i + 1) for i in range(count - 1)]
    backward = [(target, source) for source, target in forward]
    last = block.shape[dim]
    low = lax.ppermute(lax.slice_in_dim(block, last - 1, last, axis=dim), axis, forward)
    high = lax.ppermute(lax.slice_in_dim(block, 0, 1, axis=dim), axis, backward)
    return (low, high)


def advance(present, courant_numbers, tracer_slope):
    change = 0.0
    ends = [faces(present, axis, dim) for axis, dim in (("lev", 1), ("row", 2), ("mem", 3))]
    for at, (low, high) in enumerate(ends):
        dim = at + 1
        size = present.shape[dim]
        behind = jnp.concatenate([low, lax.slice_in_dim(present, 0, size - 1, axis=dim)], axis=dim)
        forward = jnp.concatenate([lax.slice_in_dim(present, 1, size, axis=dim), high], axis=dim)
        velocity = courant_numbers[at]
        change = change + (
            jnp.maximum(velocity, 0.0) * (present - behind)
            + jnp.minimum(velocity, 0.0) * (forward - present)
        )
    shifted = present - change
    source = present[0] * tracer_slope[0] + present[1] * tracer_slope[1]
    return jnp.concatenate([shifted[:2], shifted[2:] - source[None]], axis=0)


def on_device(
    control_fields, perturbations, column_taper, row_taper, courant_numbers, tracer_slope
):
    member_count, level_count, row_count, column_count = control_fields.shape
    field_count = member_count * level_count
    mem_count = lax.axis_size("mem")
    mem_at = lax.axis_index("mem")
    width = column_count // mem_count
    own_block = lax.dynamic_slice_in_dim(column_taper, mem_at * width, width, 1)
    taper_columns = lax.all_gather(own_block, "row", axis=0, tiled=True)
    row_whole = lax.all_gather(row_taper, "row", axis=0, tiled=True)
    fields = control_fields.reshape(field_count, row_count, column_count)
    tapered = jnp.einsum(
        "ij,fjc->fic",
        row_whole,
        lax.all_to_all(fields, "row", split_axis=2, concat_axis=1, tiled=True),
        preferred_element_type=jnp.float32,
    )
    tapered = lax.all_to_all(
        tapered.astype(jnp.bfloat16), "row", split_axis=1, concat_axis=2, tiled=True
    )
    weighted = 0.0
    for shift in range(mem_count):
        ring = [(i, (i + shift) % mem_count) for i in range(mem_count)]
        target = lax.rem(mem_at + shift, mem_count)
        part = lax.dynamic_slice_in_dim(perturbations, target * width, width, 4)
        half = tapered
        if shift:
            part = lax.ppermute(part, "mem", ring)
            half = lax.ppermute(half, "mem", ring)
        localized = jnp.dot(
            half.reshape(field_count * row_count, column_count),
            taper_columns,
            preferred_element_type=jnp.float32,
        ).reshape(member_count, level_count, row_count, width)
        for m in range(member_count):
            weighted = weighted + part[:, m].astype(jnp.float32) * localized[m][None]
    present = weighted
    for advect_step in range(STEPS):
        present = advance(present, courant_numbers, tracer_slope)
    return present


def solution(mesh):
    placed = (
        P("mem", "lev", "row", None),
        P(None, "mem", "lev", "row", None),
        P("row", None),
        P("row", None),
        P(None, "lev", "row", "mem"),
        P(None, "lev", "row", "mem"),
    )
    return jax.shard_map(
        on_device,
        mesh=mesh,
        in_specs=placed,
        out_specs=P(None, "lev", "row", "mem"),
        check_vma=False,
    )
```

profile of v0, /device:TPU:13, one launch (start us, length us, event | category | flops | bytes accessed | tf_op | source)
XLA Modules:
  0.0 221.7 jit_solution(6026272361632896268)
XLA Ops:
  8.6 4.2 %copy.27 = bf16[6,32,2048]{1,0,2:T(8,128)(2,1)} copy(bf16[6,32,2048]{2,1,0:T(8,128)(2,1)S(1)} %bitcast.79) | data formatting | bytes 1572864 | tf_op jit(solution)/shard_map/reshape | solution.py:48
  12.9 5.7 %reshape.36 = bf16[8,2,24576]{2,1,0:T(2,128)(2,1)} reshape(bf16[2048,6,32]{2,1,0:T(8,128)(2,1)} %bitcast.70) | data formatting | bytes 1572864
  18.6 5.8 %all-to-all-start = ((bf16[8,2,24576]{2,1,0:T(2,128)(2,1)}), bf16[8,2,24576]{2,1,0:T(2,128)(2,1)S(1)}, u32[]{:S(2)}, u32[]{:S(2)}) async-start(bf16[8,2,24576]{2,1,0:T(2,128)(2,1)} %reshape.36), calls=%async_computation | async-start | bytes 1572864 | tf_op jit(solution)/shard_map/all_to_all | solution.py:52
  24.4 47.8 %all_gather.6 = bf16[256,256]{1,0:T(8,128)(2,1)S(1)} all-gather(bf16[32,256]{1,0:T(8,128)(2,1)S(1)} %copy-done.6), channel_id=1, replica_groups=mesh['row'=8,'mem'=2,'lev'=2] {'row'}, dimensions={0}, use_global_device_ids=true | all-gather | bytes 147456 | tf_op jit(solution)/shard_map/all_gather | solution.py:47
  72.2 4.2 %reshape.37 = bf16[2048,6,32]{2,1,0:T(8,128)(2,1)} reshape(bf16[8,2,24576]{2,1,0:T(2,128)(2,1)S(1)} %all-to-all-done) | data formatting | bytes 1572864
  76.4 4.1 %copy.29 = bf16[6,8,32,256]{3,2,1,0:T(8,128)(2,1)S(1)} copy(bf16[6,8,32,256]{2,0,3,1:T(8,128)(2,1)} %bitcast.69) | data formatting | bytes 1572864 | tf_op jit(solution)/shard_map/all_to_all | solution.py:52
  80.9 1.8 copy.31
  82.7 4.6 %all-to-all-start.1 = ((bf16[6,256,256]{2,0,1:T(8,128)(2,1)}), bf16[6,256,256]{2,0,1:T(8,128)(2,1)S(1)}, u32[]{:S(2)}, u32[]{:S(2)}) async-start(bf16[6,256,256]{2,0,1:T(8,128)(2,1)} %copy.31), calls=%async_computation.1 | async-start | bytes 2097152 | tf_op jit(solution)/shard_map/all_to_all | solution.py:55
  87.2 1.4 constant_dynamic-slice_fusion
  89.8 6.7 %collective-permute-start = (bf16[3,2,3,32,1024]{4,3,2,0,1:T(8,128)(2,1)}, bf16[3,2,3,32,1024]{4,3,2,0,1:T(8,128)(2,1)}, u32[]{:S(2)}, u32[]{:S(2)}) collective-permute-start(bf16[3,2,3,32,1024]{4,3,2,0,1:T(8,128)(2,1)} %copy.44), channel_id=1, source_target_pairs={{0,2},{2,0},{1,3},{3,1},{4,6},{6,4},{5,7},{7,5},{8,10},{10,8},{9,1... | collective-permute-start | bytes 3538952 | tf_op jit(solution)/shard_map/ppermute | solution.py:65
  96.4 21.4 %all-to-all-done.1 = bf16[6,256,256]{2,0,1:T(8,128)(2,1)S(1)} async-done(((bf16[6,256,256]{2,0,1:T(8,128)(2,1)}), bf16[6,256,256]{2,0,1:T(8,128)(2,1)S(1)}, u32[]{:S(2)}, u32[]{:S(2)}) %all-to-all-start.1) | async-done | bytes 786464 | tf_op jit(solution)/shard_map/all_to_all | solution.py:55
  119.6 1.5 collective-permute-start.1
  121.0 1.6 maximum_bitcast_fusion.2
  123.8 3.6 %fusion.105 = f32[192,1024]{1,0:T(8,128)S(1)} fusion(bf16[192,2048]{1,0:T(8,128)(2,1)} %bitcast.74, bf16[2048,1024]{1,0:T(8,128)(2,1)} %all-gather.2.cloned.1.call-done), kind=kOutput, calls=%fused_computation.230 | convolution fusion | flops 805306368 | bytes 5767168 | tf_op jit(solution)/shard_map/dot_general | solution.py:67
  127.5 2.3 %fusion.106 = f32[192,1024]{1,0:T(8,128)S(1)} fusion(bf16[192,2048]{1,0:T(8,128)(2,1)} %bitcast.17, bf16[2048,1024]{1,0:T(8,128)(2,1)S(1)} %copy-done.2), kind=kOutput, calls=%fused_computation.231 | convolution fusion | flops 805306368 | bytes 5767168 | tf_op jit(solution)/shard_map/dot_general | solution.py:67
  129.9 1.8 fusion.61
  132.6 1.9 collective-permute-start.7
  134.5 2.2 collective-permute-start.3
  136.7 1.3 collective-permute-start.2
  138.1 4.9 %collective-permute-start.5 = (f32[3,3,1,1024]{3,2,1,0:T(1,128)S(1)}, f32[3,3,1,1024]{3,2,1,0:T(1,128)S(1)}, u32[]{:S(2)}, u32[]{:S(2)}) collective-permute-start(f32[3,3,1,1024]{3,2,1,0:T(1,128)S(1)} %get-tuple-element.53), channel_id=1, source_target_pairs={{4,0},{8,4},{12,8},{16,12},{20,16},{24,20},{28,24},{5,1},{9,5},{13... | collective-permute-start | bytes 110600 | tf_op jit(solution)/shard_map/ppermute | solution.py:15
  143.0 1.9 collective-permute-start.4
  145.0 1.3 collective-permute-start.6
  146.4 1.8 collective-permute-done.6
  149.6 1.6 fusion.17
  153.0 2.4 %collective-permute-start.13 = (f32[3,3,32,1]{3,2,1,0:T(8,128)S(1)}, f32[3,3,32,1]{3,2,1,0:T(8,128)S(1)}, u32[]{:S(2)}, u32[]{:S(2)}) collective-permute-start(f32[3,3,32,1]{3,2,1,0:T(8,128)S(1)} %get-tuple-element.31), channel_id=1, source_target_pairs={{2,0},{3,1},{6,4},{7,5},{10,8},{11,9},{14,12},{15,13},{18,16},{19,... | collective-permute-start | bytes 3464 | tf_op jit(solution)/shard_map/ppermute | solution.py:15
  155.4 3.9 %collective-permute-start.9 = (f32[3,1,32,1024]{3,2,1,0:T(8,128)S(1)}, f32[3,1,32,1024]{3,2,1,0:T(8,128)S(1)}, u32[]{:S(2)}, u32[]{:S(2)}) collective-permute-start(f32[3,1,32,1024]{3,2,1,0:T(8,128)S(1)} %get-tuple-element.39), channel_id=1, source_target_pairs={{1,0},{3,2},{5,4},{7,6},{9,8},{11,10},{13,12},{15,14},{17,16},{19,... | collective-permute-start | bytes 1179656 | tf_op jit(solution)/shard_map/ppermute | solution.py:15
  159.3 1.3 collective-permute-start.8
  161.1 2.7 %collective-permute-start.11 = (f32[3,3,1,1024]{3,2,1,0:T(1,128)S(1)}, f32[3,3,1,1024]{3,2,1,0:T(1,128)S(1)}, u32[]{:S(2)}, u32[]{:S(2)}) collective-permute-start(f32[3,3,1,1024]{3,2,1,0:T(1,128)S(1)} %get-tuple-element.35), channel_id=1, source_target_pairs={{4,0},{8,4},{12,8},{16,12},{20,16},{24,20},{28,24},{5,1},{9,5},{13... | collective-permute-start | bytes 110600 | tf_op jit(solution)/shard_map/ppermute | solution.py:15
  163.8 2.6 %collective-permute-start.10 = (f32[3,3,1,1024]{3,2,1,0:T(1,128)S(1)}, f32[3,3,1,1024]{3,2,1,0:T(1,128)S(1)}, u32[]{:S(2)}, u32[]{:S(2)}) collective-permute-start(f32[3,3,1,1024]{3,2,1,0:T(1,128)S(1)} %get-tuple-element.36), channel_id=1, source_target_pairs={{0,4},{4,8},{8,12},{12,16},{16,20},{20,24},{24,28},{1,5},{5,9},{9,... | collective-permute-start | bytes 110600 | tf_op jit(solution)/shard_map/ppermute | solution.py:14
  166.4 1.5 collective-permute-start.12
  168.1 1.6 collective-permute-done.12
  169.7 2.5 %collective-permute-done.8 = f32[3,1,32,1024]{3,2,1,0:T(8,128)S(1)} collective-permute-done((f32[3,1,32,1024]{3,2,1,0:T(8,128)S(1)}, f32[3,1,32,1024]{3,2,1,0:T(8,128)S(1)}, u32[]{:S(2)}, u32[]{:S(2)}) %collective-permute-start.8) | collective-permute-done | bytes 393248 | tf_op jit(solution)/shard_map/ppermute | solution.py:14
  172.2 1.6 fusion.29
  174.5 2.4 %collective-permute-start.19 = (f32[3,3,32,1]{3,2,1,0:T(8,128)S(1)}, f32[3,3,32,1]{3,2,1,0:T(8,128)S(1)}, u32[]{:S(2)}, u32[]{:S(2)}) collective-permute-start(f32[3,3,32,1]{3,2,1,0:T(8,128)S(1)} %get-tuple-element.19), channel_id=1, source_target_pairs={{2,0},{3,1},{6,4},{7,5},{10,8},{11,9},{14,12},{15,13},{18,16},{19,... | collective-permute-start | bytes 3464 | tf_op jit(solution)/shard_map/ppermute | solution.py:15
  176.9 2.1 collective-permute-start.15
  180.8 2.7 %collective-permute-start.17 = (f32[3,3,1,1024]{3,2,1,0:T(1,128)S(1)}, f32[3,3,1,1024]{3,2,1,0:T(1,128)S(1)}, u32[]{:S(2)}, u32[]{:S(2)}) collective-permute-start(f32[3,3,1,1024]{3,2,1,0:T(1,128)S(1)} %get-tuple-element.23), channel_id=1, source_target_pairs={{4,0},{8,4},{12,8},{16,12},{20,16},{24,20},{28,24},{5,1},{9,5},{13... | collective-permute-start | bytes 110600 | tf_op jit(solution)/shard_map/ppermute | solution.py:15
  183.5 2.6 %collective-permute-start.16 = (f32[3,3,1,1024]{3,2,1,0:T(1,128)S(1)}, f32[3,3,1,1024]{3,2,1,0:T(1,128)S(1)}, u32[]{:S(2)}, u32[]{:S(2)}) collective-permute-start(f32[3,3,1,1024]{3,2,1,0:T(1,128)S(1)} %get-tuple-element.24), channel_id=1, source_target_pairs={{0,4},{4,8},{8,12},{12,16},{16,20},{20,24},{24,28},{1,5},{5,9},{9,... | collective-permute-start | bytes 110600 | tf_op jit(solution)/shard_map/ppermute | solution.py:14
  187.6 1.8 collective-permute-done.18
  189.4 2.5 %collective-permute-done.14 = f32[3,1,32,1024]{3,2,1,0:T(8,128)S(1)} collective-permute-done((f32[3,1,32,1024]{3,2,1,0:T(8,128)S(1)}, f32[3,1,32,1024]{3,2,1,0:T(8,128)S(1)}, u32[]{:S(2)}, u32[]{:S(2)}) %collective-permute-start.14) | collective-permute-done | bytes 393248 | tf_op jit(solution)/shard_map/ppermute | solution.py:14
  191.9 1.6 fusion.41
  194.2 2.4 %collective-permute-start.25 = (f32[3,3,32,1]{3,2,1,0:T(8,128)S(1)}, f32[3,3,32,1]{3,2,1,0:T(8,128)S(1)}, u32[]{:S(2)}, u32[]{:S(2)}) collective-permute-start(f32[3,3,32,1]{3,2,1,0:T(8,128)S(1)} %get-tuple-element.7), channel_id=1, source_target_pairs={{2,0},{3,1},{6,4},{7,5},{10,8},{11,9},{14,12},{15,13},{18,16},{19,... | collective-permute-start | bytes 3464 | tf_op jit(solution)/shard_map/ppermute | solution.py:15
  196.7 2.1 collective-permute-start.21
  200.6 2.7 %collective-permute-start.23 = (f32[3,3,1,1024]{3,2,1,0:T(1,128)S(1)}, f32[3,3,1,1024]{3,2,1,0:T(1,128)S(1)}, u32[]{:S(2)}, u32[]{:S(2)}) collective-permute-start(f32[3,3,1,1024]{3,2,1,0:T(1,128)S(1)} %get-tuple-element.11), channel_id=1, source_target_pairs={{4,0},{8,4},{12,8},{16,12},{20,16},{24,20},{28,24},{5,1},{9,5},{13... | collective-permute-start | bytes 110600 | tf_op jit(solution)/shard_map/ppermute | solution.py:15
  203.2 2.6 %collective-permute-start.22 = (f32[3,3,1,1024]{3,2,1,0:T(1,128)S(1)}, f32[3,3,1,1024]{3,2,1,0:T(1,128)S(1)}, u32[]{:S(2)}, u32[]{:S(2)}) collective-permute-start(f32[3,3,1,1024]{3,2,1,0:T(1,128)S(1)} %get-tuple-element.12), channel_id=1, source_target_pairs={{0,4},{4,8},{8,12},{12,16},{16,20},{20,24},{24,28},{1,5},{5,9},{9,... | collective-permute-start | bytes 110600 | tf_op jit(solution)/shard_map/ppermute | solution.py:14
  205.9 1.3 collective-permute-start.24
  207.4 1.8 collective-permute-done.24
  209.1 2.5 %collective-permute-done.20 = f32[3,1,32,1024]{3,2,1,0:T(8,128)S(1)} collective-permute-done((f32[3,1,32,1024]{3,2,1,0:T(8,128)S(1)}, f32[3,1,32,1024]{3,2,1,0:T(8,128)S(1)}, u32[]{:S(2)}, u32[]{:S(2)}) %collective-permute-start.20) | collective-permute-done | bytes 393248 | tf_op jit(solution)/shard_map/ppermute | solution.py:14
  211.7 1.6 fusion.53
  (81 shorter events, 19.7 us)
Async XLA Ops:
  6.5 1.2 copy-start
  6.5 2.1 copy-start.5
  6.5 117.3 %all-gather.2.cloned.1.call-start = ((), (), s32[]{:S(2)}) async-start(), calls=%async_computation.2 | async-start | bytes 4718592 | tf_op jit(solution)/shard_map/all_gather | solution.py:46
  18.6 5.8 %copy-start.6 = (bf16[32,256]{1,0:T(8,128)(2,1)S(1)}, bf16[32,256]{1,0:T(8,128)(2,1)}, u32[]{:S(2)}) copy-start(bf16[32,256]{1,0:T(8,128)(2,1)} %param.9) | copy-start | bytes 49156
  18.6 53.6 %all-to-all-start = ((bf16[8,2,24576]{2,1,0:T(2,128)(2,1)}), bf16[8,2,24576]{2,1,0:T(2,128)(2,1)S(1)}, u32[]{:S(2)}, u32[]{:S(2)}) async-start(bf16[8,2,24576]{2,1,0:T(2,128)(2,1)} %reshape.36), calls=%async_computation | async-start | bytes 1572864 | tf_op jit(solution)/shard_map/all_to_all | solution.py:52
  82.7 35.2 %all-to-all-start.1 = ((bf16[6,256,256]{2,0,1:T(8,128)(2,1)}), bf16[6,256,256]{2,0,1:T(8,128)(2,1)S(1)}, u32[]{:S(2)}, u32[]{:S(2)}) async-start(bf16[6,256,256]{2,0,1:T(8,128)(2,1)} %copy.31), calls=%async_computation.1 | async-start | bytes 2097152 | tf_op jit(solution)/shard_map/all_to_all | solution.py:55
  89.8 40.1 %collective-permute-start = (bf16[3,2,3,32,1024]{4,3,2,0,1:T(8,128)(2,1)}, bf16[3,2,3,32,1024]{4,3,2,0,1:T(8,128)(2,1)}, u32[]{:S(2)}, u32[]{:S(2)}) collective-permute-start(bf16[3,2,3,32,1024]{4,3,2,0,1:T(8,128)(2,1)} %copy.44), channel_id=1, source_target_pairs={{0,2},{2,0},{1,3},{3,1},{4,6},{6,4},{5,7},{7,5},{8,10},{10,8},{9,1... | collective-permute-start | bytes 3538952 | tf_op jit(solution)/shard_map/ppermute | solution.py:65
  119.6 7.9 %collective-permute-start.1 = (bf16[6,32,2048]{2,1,0:T(8,128)(2,1)}, bf16[6,32,2048]{2,1,0:T(8,128)(2,1)}, u32[]{:S(2)}, u32[]{:S(2)}) collective-permute-start(bf16[6,32,2048]{2,1,0:T(8,128)(2,1)} %all_to_all.33), channel_id=1, source_target_pairs={{0,2},{2,0},{1,3},{3,1},{4,6},{6,4},{5,7},{7,5},{8,10},{10,8},{9,1... | collective-permute-start | bytes 2359304 | tf_op jit(solution)/shard_map/ppermute | solution.py:66
  123.8 3.7 %copy-start.2 = (bf16[2048,1024]{1,0:T(8,128)(2,1)S(1)}, bf16[2048,1024]{1,0:T(8,128)(2,1)}, u32[]{:S(2)}) copy-start(bf16[2048,1024]{1,0:T(8,128)(2,1)} %all-gather.2.cloned.1.call-done) | copy-start | bytes 12582916
  127.5 2.4 %copy-start.4 = (bf16[3,2,3,32,2048]{4,3,2,1,0:T(8,128)(2,1)S(1)}, bf16[3,2,3,32,2048]{4,3,2,1,0:T(8,128)(2,1)}, u32[]{:S(2)}) copy-start(bf16[3,2,3,32,2048]{4,3,2,1,0:T(8,128)(2,1)} %param.7) | copy-start | bytes 7077892
  132.6 12.4 %collective-permute-start.7 = (f32[3,3,32,1]{3,2,1,0:T(8,128)S(1)}, f32[3,3,32,1]{3,2,1,0:T(8,128)S(1)}, u32[]{:S(2)}, u32[]{:S(2)}) collective-permute-start(f32[3,3,32,1]{3,2,1,0:T(8,128)S(1)} %get-tuple-element.49), channel_id=1, source_target_pairs={{2,0},{3,1},{6,4},{7,5},{10,8},{11,9},{14,12},{15,13},{18,16},{19,... | collective-permute-start | bytes 3464 | tf_op jit(solution)/shard_map/ppermute | solution.py:15
  134.5 14.1 %collective-permute-start.3 = (f32[3,1,32,1024]{3,2,1,0:T(8,128)S(1)}, f32[3,1,32,1024]{3,2,1,0:T(8,128)S(1)}, u32[]{:S(2)}, u32[]{:S(2)}) collective-permute-start(f32[3,1,32,1024]{3,2,1,0:T(8,128)S(1)} %get-tuple-element.57), channel_id=1, source_target_pairs={{1,0},{3,2},{5,4},{7,6},{9,8},{11,10},{13,12},{15,14},{17,16},{19,... | collective-permute-start | bytes 1179656 | tf_op jit(solution)/shard_map/ppermute | solution.py:15
  136.7 12.9 %collective-permute-start.2 = (f32[3,1,32,1024]{3,2,1,0:T(8,128)S(1)}, f32[3,1,32,1024]{3,2,1,0:T(8,128)S(1)}, u32[]{:S(2)}, u32[]{:S(2)}) collective-permute-start(f32[3,1,32,1024]{3,2,1,0:T(8,128)S(1)} %get-tuple-element.58), channel_id=1, source_target_pairs={{0,1},{2,3},{4,5},{6,7},{8,9},{10,11},{12,13},{14,15},{16,17},{18,... | collective-permute-start | bytes 1179656 | tf_op jit(solution)/shard_map/ppermute | solution.py:14
  138.1 10.1 %collective-permute-start.5 = (f32[3,3,1,1024]{3,2,1,0:T(1,128)S(1)}, f32[3,3,1,1024]{3,2,1,0:T(1,128)S(1)}, u32[]{:S(2)}, u32[]{:S(2)}) collective-permute-start(f32[3,3,1,1024]{3,2,1,0:T(1,128)S(1)} %get-tuple-element.53), channel_id=1, source_target_pairs={{4,0},{8,4},{12,8},{16,12},{20,16},{24,20},{28,24},{5,1},{9,5},{13... | collective-permute-start | bytes 110600 | tf_op jit(solution)/shard_map/ppermute | solution.py:15
  143.0 5.6 %collective-permute-start.4 = (f32[3,3,1,1024]{3,2,1,0:T(1,128)S(1)}, f32[3,3,1,1024]{3,2,1,0:T(1,128)S(1)}, u32[]{:S(2)}, u32[]{:S(2)}) collective-permute-start(f32[3,3,1,1024]{3,2,1,0:T(1,128)S(1)} %get-tuple-element.54), channel_id=1, source_target_pairs={{0,4},{4,8},{8,12},{12,16},{16,20},{20,24},{24,28},{1,5},{5,9},{9,... | collective-permute-start | bytes 110600 | tf_op jit(solution)/shard_map/ppermute | solution.py:14
  145.0 3.3 %collective-permute-start.6 = (f32[3,3,32,1]{3,2,1,0:T(8,128)S(1)}, f32[3,3,32,1]{3,2,1,0:T(8,128)S(1)}, u32[]{:S(2)}, u32[]{:S(2)}) collective-permute-start(f32[3,3,32,1]{3,2,1,0:T(8,128)S(1)} %get-tuple-element.50), channel_id=1, source_target_pairs={{0,2},{1,3},{4,6},{5,7},{8,10},{9,11},{12,14},{13,15},{16,18},{17,... | collective-permute-start | bytes 3464 | tf_op jit(solution)/shard_map/ppermute | solution.py:14
  151.2 1.1 copy-start.3
  153.0 13.4 %collective-permute-start.13 = (f32[3,3,32,1]{3,2,1,0:T(8,128)S(1)}, f32[3,3,32,1]{3,2,1,0:T(8,128)S(1)}, u32[]{:S(2)}, u32[]{:S(2)}) collective-permute-start(f32[3,3,32,1]{3,2,1,0:T(8,128)S(1)} %get-tuple-element.31), channel_id=1, source_target_pairs={{2,0},{3,1},{6,4},{7,5},{10,8},{11,9},{14,12},{15,13},{18,16},{19,... | collective-permute-start | bytes 3464 | tf_op jit(solution)/shard_map/ppermute | solution.py:15
  155.4 14.3 %collective-permute-start.9 = (f32[3,1,32,1024]{3,2,1,0:T(8,128)S(1)}, f32[3,1,32,1024]{3,2,1,0:T(8,128)S(1)}, u32[]{:S(2)}, u32[]{:S(2)}) collective-permute-start(f32[3,1,32,1024]{3,2,1,0:T(8,128)S(1)} %get-tuple-element.39), channel_id=1, source_target_pairs={{1,0},{3,2},{5,4},{7,6},{9,8},{11,10},{13,12},{15,14},{17,16},{19,... | collective-permute-start | bytes 1179656 | tf_op jit(solution)/shard_map/ppermute | solution.py:15
  159.3 12.9 %collective-permute-start.8 = (f32[3,1,32,1024]{3,2,1,0:T(8,128)S(1)}, f32[3,1,32,1024]{3,2,1,0:T(8,128)S(1)}, u32[]{:S(2)}, u32[]{:S(2)}) collective-permute-start(f32[3,1,32,1024]{3,2,1,0:T(8,128)S(1)} %get-tuple-element.40), channel_id=1, source_target_pairs={{0,1},{2,3},{4,5},{6,7},{8,9},{10,11},{12,13},{14,15},{16,17},{18,... | collective-permute-start | bytes 1179656 | tf_op jit(solution)/shard_map/ppermute | solution.py:14
  161.1 8.6 %collective-permute-start.11 = (f32[3,3,1,1024]{3,2,1,0:T(1,128)S(1)}, f32[3,3,1,1024]{3,2,1,0:T(1,128)S(1)}, u32[]{:S(2)}, u32[]{:S(2)}) collective-permute-start(f32[3,3,1,1024]{3,2,1,0:T(1,128)S(1)} %get-tuple-element.35), channel_id=1, source_target_pairs={{4,0},{8,4},{12,8},{16,12},{20,16},{24,20},{28,24},{5,1},{9,5},{13... | collective-permute-start | bytes 110600 | tf_op jit(solution)/shard_map/ppermute | solution.py:15
  163.8 5.9 %collective-permute-start.10 = (f32[3,3,1,1024]{3,2,1,0:T(1,128)S(1)}, f32[3,3,1,1024]{3,2,1,0:T(1,128)S(1)}, u32[]{:S(2)}, u32[]{:S(2)}) collective-permute-start(f32[3,3,1,1024]{3,2,1,0:T(1,128)S(1)} %get-tuple-element.36), channel_id=1, source_target_pairs={{0,4},{4,8},{8,12},{12,16},{16,20},{20,24},{24,28},{1,5},{5,9},{9,... | collective-permute-start | bytes 110600 | tf_op jit(solution)/shard_map/ppermute | solution.py:14
  166.4 3.3 %collective-permute-start.12 = (f32[3,3,32,1]{3,2,1,0:T(8,128)S(1)}, f32[3,3,32,1]{3,2,1,0:T(8,128)S(1)}, u32[]{:S(2)}, u32[]{:S(2)}) collective-permute-start(f32[3,3,32,1]{3,2,1,0:T(8,128)S(1)} %get-tuple-element.32), channel_id=1, source_target_pairs={{0,2},{1,3},{4,6},{5,7},{8,10},{9,11},{12,14},{13,15},{16,18},{17,... | collective-permute-start | bytes 3464 | tf_op jit(solution)/shard_map/ppermute | solution.py:14
  174.5 11.6 %collective-permute-start.19 = (f32[3,3,32,1]{3,2,1,0:T(8,128)S(1)}, f32[3,3,32,1]{3,2,1,0:T(8,128)S(1)}, u32[]{:S(2)}, u32[]{:S(2)}) collective-permute-start(f32[3,3,32,1]{3,2,1,0:T(8,128)S(1)} %get-tuple-element.19), channel_id=1, source_target_pairs={{2,0},{3,1},{6,4},{7,5},{10,8},{11,9},{14,12},{15,13},{18,16},{19,... | collective-permute-start | bytes 3464 | tf_op jit(solution)/shard_map/ppermute | solution.py:15
  176.9 12.5 %collective-permute-start.15 = (f32[3,1,32,1024]{3,2,1,0:T(8,128)S(1)}, f32[3,1,32,1024]{3,2,1,0:T(8,128)S(1)}, u32[]{:S(2)}, u32[]{:S(2)}) collective-permute-start(f32[3,1,32,1024]{3,2,1,0:T(8,128)S(1)} %get-tuple-element.27), channel_id=1, source_target_pairs={{1,0},{3,2},{5,4},{7,6},{9,8},{11,10},{13,12},{15,14},{17,16},{19,... | collective-permute-start | bytes 1179656 | tf_op jit(solution)/shard_map/ppermute | solution.py:15
  179.0 12.9 %collective-permute-start.14 = (f32[3,1,32,1024]{3,2,1,0:T(8,128)S(1)}, f32[3,1,32,1024]{3,2,1,0:T(8,128)S(1)}, u32[]{:S(2)}, u32[]{:S(2)}) collective-permute-start(f32[3,1,32,1024]{3,2,1,0:T(8,128)S(1)} %get-tuple-element.28), channel_id=1, source_target_pairs={{0,1},{2,3},{4,5},{6,7},{8,9},{10,11},{12,13},{14,15},{16,17},{18,... | collective-permute-start | bytes 1179656 | tf_op jit(solution)/shard_map/ppermute | solution.py:14
  180.8 8.6 %collective-permute-start.17 = (f32[3,3,1,1024]{3,2,1,0:T(1,128)S(1)}, f32[3,3,1,1024]{3,2,1,0:T(1,128)S(1)}, u32[]{:S(2)}, u32[]{:S(2)}) collective-permute-start(f32[3,3,1,1024]{3,2,1,0:T(1,128)S(1)} %get-tuple-element.23), channel_id=1, source_target_pairs={{4,0},{8,4},{12,8},{16,12},{20,16},{24,20},{28,24},{5,1},{9,5},{13... | collective-permute-start | bytes 110600 | tf_op jit(solution)/shard_map/ppermute | solution.py:15
  183.5 5.9 %collective-permute-start.16 = (f32[3,3,1,1024]{3,2,1,0:T(1,128)S(1)}, f32[3,3,1,1024]{3,2,1,0:T(1,128)S(1)}, u32[]{:S(2)}, u32[]{:S(2)}) collective-permute-start(f32[3,3,1,1024]{3,2,1,0:T(1,128)S(1)} %get-tuple-element.24), channel_id=1, source_target_pairs={{0,4},{4,8},{8,12},{12,16},{16,20},{20,24},{24,28},{1,5},{5,9},{9,... | collective-permute-start | bytes 110600 | tf_op jit(solution)/shard_map/ppermute | solution.py:14
  186.1 3.3 %collective-permute-start.18 = (f32[3,3,32,1]{3,2,1,0:T(8,128)S(1)}, f32[3,3,32,1]{3,2,1,0:T(8,128)S(1)}, u32[]{:S(2)}, u32[]{:S(2)}) collective-permute-start(f32[3,3,32,1]{3,2,1,0:T(8,128)S(1)} %get-tuple-element.20), channel_id=1, source_target_pairs={{0,2},{1,3},{4,6},{5,7},{8,10},{9,11},{12,14},{13,15},{16,18},{17,... | collective-permute-start | bytes 3464 | tf_op jit(solution)/shard_map/ppermute | solution.py:14
  194.2 11.6 %collective-permute-start.25 = (f32[3,3,32,1]{3,2,1,0:T(8,128)S(1)}, f32[3,3,32,1]{3,2,1,0:T(8,128)S(1)}, u32[]{:S(2)}, u32[]{:S(2)}) collective-permute-start(f32[3,3,32,1]{3,2,1,0:T(8,128)S(1)} %get-tuple-element.7), channel_id=1, source_target_pairs={{2,0},{3,1},{6,4},{7,5},{10,8},{11,9},{14,12},{15,13},{18,16},{19,... | collective-permute-start | bytes 3464 | tf_op jit(solution)/shard_map/ppermute | solution.py:15
  196.7 12.5 %collective-permute-start.21 = (f32[3,1,32,1024]{3,2,1,0:T(8,128)S(1)}, f32[3,1,32,1024]{3,2,1,0:T(8,128)S(1)}, u32[]{:S(2)}, u32[]{:S(2)}) collective-permute-start(f32[3,1,32,1024]{3,2,1,0:T(8,128)S(1)} %get-tuple-element.15), channel_id=1, source_target_pairs={{1,0},{3,2},{5,4},{7,6},{9,8},{11,10},{13,12},{15,14},{17,16},{19,... | collective-permute-start | bytes 1179656 | tf_op jit(solution)/shard_map/ppermute | solution.py:15
  198.7 12.9 %collective-permute-start.20 = (f32[3,1,32,1024]{3,2,1,0:T(8,128)S(1)}, f32[3,1,32,1024]{3,2,1,0:T(8,128)S(1)}, u32[]{:S(2)}, u32[]{:S(2)}) collective-permute-start(f32[3,1,32,1024]{3,2,1,0:T(8,128)S(1)} %get-tuple-element.16), channel_id=1, source_target_pairs={{0,1},{2,3},{4,5},{6,7},{8,9},{10,11},{12,13},{14,15},{16,17},{18,... | collective-permute-start | bytes 1179656 | tf_op jit(solution)/shard_map/ppermute | solution.py:14
  200.6 8.6 %collective-permute-start.23 = (f32[3,3,1,1024]{3,2,1,0:T(1,128)S(1)}, f32[3,3,1,1024]{3,2,1,0:T(1,128)S(1)}, u32[]{:S(2)}, u32[]{:S(2)}) collective-permute-start(f32[3,3,1,1024]{3,2,1,0:T(1,128)S(1)} %get-tuple-element.11), channel_id=1, source_target_pairs={{4,0},{8,4},{12,8},{16,12},{20,16},{24,20},{28,24},{5,1},{9,5},{13... | collective-permute-start | bytes 110600 | tf_op jit(solution)/shard_map/ppermute | solution.py:15
  203.2 5.9 %collective-permute-start.22 = (f32[3,3,1,1024]{3,2,1,0:T(1,128)S(1)}, f32[3,3,1,1024]{3,2,1,0:T(1,128)S(1)}, u32[]{:S(2)}, u32[]{:S(2)}) collective-permute-start(f32[3,3,1,1024]{3,2,1,0:T(1,128)S(1)} %get-tuple-element.12), channel_id=1, source_target_pairs={{0,4},{4,8},{8,12},{12,16},{16,20},{20,24},{24,28},{1,5},{5,9},{9,... | collective-permute-start | bytes 110600 | tf_op jit(solution)/shard_map/ppermute | solution.py:14
  205.9 3.3 %collective-permute-start.24 = (f32[3,3,32,1]{3,2,1,0:T(8,128)S(1)}, f32[3,3,32,1]{3,2,1,0:T(8,128)S(1)}, u32[]{:S(2)}, u32[]{:S(2)}) collective-permute-start(f32[3,3,32,1]{3,2,1,0:T(8,128)S(1)} %get-tuple-element.8), channel_id=1, source_target_pairs={{0,2},{1,3},{4,6},{5,7},{8,10},{9,11},{12,14},{13,15},{16,18},{17,... | collective-permute-start | bytes 3464 | tf_op jit(solution)/shard_map/ppermute | solution.py:14
  213.4 1.4 copy-start.1
Sparse Core Ops, SparseCore 0:
  9.5 94.2 all-gather.1
where the time goes:
time: 223 us; the launch traced here: 222 us
  starting transfers between devices  71.2 us (32%)
  blocking collectives  47.8 us (21%)
  waiting for transfers between devices  37.3 us (17%)
  local copies, waits for them, and re-layouts  30.3 us (14%)
  other arithmetic  14.8 us (7%)
  between operations  14 us (6%)
  matrix products  6.28 us (3%)
    all_gather x1, blocking collectives, on_device(): row_whole = lax.all_gather(row_taper, 'row', axis=0, tiled=True)  47.8 us
    ppermute x12, starting transfers between devices, faces(): high = lax.ppermute(lax.slice_in_dim(block, 0, 1, axis=dim), axis, backward)  32.5 us
    all_to_all x1, waiting for transfers between devices, on_device(): lax.all_to_all(tapered.astype(jnp.bfloat16), 'row', split_axis=1, concat_...  21.4 us
    ppermute x12, starting transfers between devices, faces(): lax.ppermute(lax.slice_in_dim(block, last - 1, last, axis=dim), axis, for...  20.2 us
    ppermute x12, waiting for transfers between devices, faces(): lax.ppermute(lax.slice_in_dim(block, last - 1, last, axis=dim), axis, for...  15.8 us
    unnamed x18, local copies, waits for them, and re-layouts  14.7 us
    ppermute x1, starting transfers between devices, on_device(): part = lax.ppermute(part, 'mem', ring)  6.65 us
    sub x4, other arithmetic, advance(): shifted = present - change  6.37 us
  transfers between devices with their start and end apart: 29, of which 10 were waited for; matrix products, arithmetic and copies ran while one was open for 16% of the time, Pallas kernels for 0%

commit v1 on v0

--- a/solution.py
+++ b/solution.py
@@ -52,8 +52,14 @@
         lax.all_to_all(fields, "row", split_axis=2, concat_axis=1, tiled=True),
         preferred_element_type=jnp.float32,
     )
-    tapered = lax.all_to_all(
-        tapered.astype(jnp.bfloat16), "row", split_axis=1, concat_axis=2, tiled=True
+    tapered = jnp.concatenate(
+        lax.all_to_all(
+            jnp.stack(jnp.split(tapered.astype(jnp.bfloat16), lax.axis_size("row"), axis=1)),
+            "row",
+            0,
+            0,
+        ),
+        axis=2,
     )
     weighted = 0.0
     for shift in range(mem_count):

time: 223 us -> 216 us (0.969)
  waiting for transfers between devices: 37.3 us -> 30.4 us
    all_to_all x1, waiting for transfers between devices: 21.4 us -> 13.7 us  [on_device(): lax.all_to_all(jnp.stack(jnp.split(tapered.astype(jnp.bfloat16), lax.axis...]
    unnamed x18 -> x27, local copies, waits for them, and re-layouts: 14.7 us -> 18.2 us
  transfers between devices with their start and end apart: 29 -> 29, of which waited for: 10 -> 10; matrix products, arithmetic and copies ran while one was open for 16% -> 17% of each run, Pallas kernels for 0% -> 0%
where the time goes in v1:
time: 216 us; the launch traced here: 215 us
  starting transfers between devices  70.5 us (33%)
  blocking collectives  47.8 us (22%)
  local copies, waits for them, and re-layouts  31.1 us (14%)
  waiting for transfers between devices  30.4 us (14%)
  other arithmetic  14.8 us (7%)
  between operations  14.1 us (7%)
  matrix products  6 us (3%)
    all_gather x1, blocking collectives, on_device(): row_whole = lax.all_gather(row_taper, 'row', axis=0, tiled=True)  47.8 us
    ppermute x12, starting transfers between devices, faces(): high = lax.ppermute(lax.slice_in_dim(block, 0, 1, axis=dim), axis, backward)  30.9 us
    ppermute x12, starting transfers between devices, faces(): lax.ppermute(lax.slice_in_dim(block, last - 1, last, axis=dim), axis, for...  20.2 us
    unnamed x27, local copies, waits for them, and re-layouts  18.2 us
    ppermute x12, waiting for transfers between devices, faces(): lax.ppermute(lax.slice_in_dim(block, last - 1, last, axis=dim), axis, for...  16.6 us
    all_to_all x1, waiting for transfers between devices, on_device(): lax.all_to_all(jnp.stack(jnp.split(tapered.astype(jnp.bfloat16), lax.axis...  13.7 us
    ppermute x1, starting transfers between devices, on_device(): part = lax.ppermute(part, 'mem', ring)  6.67 us
    sub x4, other arithmetic, advance(): shifted = present - change  6.37 us
  transfers between devices with their start and end apart: 29, of which 10 were waited for; matrix products, arithmetic and copies ran while one was open for 17% of the time, Pallas kernels for 0%

profile of v1, /device:TPU:13, one launch (start us, length us, event | category | flops | bytes accessed | tf_op | source)
XLA Modules:
  0.0 214.6 jit_solution(9838749976002999155)
XLA Ops:
  8.6 4.2 %copy.22 = bf16[6,32,2048]{1,0,2:T(8,128)(2,1)} copy(bf16[6,32,2048]{2,1,0:T(8,128)(2,1)S(1)} %bitcast.108) | data formatting | bytes 1572864 | tf_op jit(solution)/shard_map/reshape | solution.py:48
  12.9 5.7 %reshape.39 = bf16[8,2,24576]{2,1,0:T(2,128)(2,1)} reshape(bf16[2048,6,32]{2,1,0:T(8,128)(2,1)} %bitcast.98) | data formatting | bytes 1572864
  18.6 5.8 %all-to-all-start = ((bf16[8,2,24576]{2,1,0:T(2,128)(2,1)}), bf16[8,2,24576]{2,1,0:T(2,128)(2,1)S(1)}, u32[]{:S(2)}, u32[]{:S(2)}) async-start(bf16[8,2,24576]{2,1,0:T(2,128)(2,1)} %reshape.39), calls=%async_computation | async-start | bytes 1572864 | tf_op jit(solution)/shard_map/all_to_all | solution.py:52
  24.4 47.8 %all_gather.6 = bf16[256,256]{1,0:T(8,128)(2,1)S(1)} all-gather(bf16[32,256]{1,0:T(8,128)(2,1)S(1)} %copy-done.7), channel_id=1, replica_groups=mesh['row'=8,'mem'=2,'lev'=2] {'row'}, dimensions={0}, use_global_device_ids=true | all-gather | bytes 147456 | tf_op jit(solution)/shard_map/all_gather | solution.py:47
  72.2 4.2 %reshape.40 = bf16[2048,6,32]{2,1,0:T(8,128)(2,1)} reshape(bf16[8,2,24576]{2,1,0:T(2,128)(2,1)S(1)} %all-to-all-done) | data formatting | bytes 1572864
  76.4 4.1 %copy.24 = bf16[6,8,32,256]{3,2,1,0:T(8,128)(2,1)S(1)} copy(bf16[6,8,32,256]{2,0,3,1:T(8,128)(2,1)} %bitcast.97) | data formatting | bytes 1572864 | tf_op jit(solution)/shard_map/all_to_all | solution.py:52
  86.0 4.5 %all-to-all-start.1 = ((bf16[8,6,32,256]{3,2,1,0:T(8,128)(2,1)}), bf16[8,6,32,256]{3,2,1,0:T(8,128)(2,1)S(1)}, u32[]{:S(2)}, u32[]{:S(2)}) async-start(bf16[8,6,32,256]{3,2,1,0:T(8,128)(2,1)} %fusion.91), calls=%async_computation.1 | async-start | bytes 1572864 | tf_op jit(solution)/shard_map/all_to_all | solution.py:56
  91.8 6.7 %collective-permute-start = (bf16[3,2,3,32,1024]{4,3,2,0,1:T(8,128)(2,1)}, bf16[3,2,3,32,1024]{4,3,2,0,1:T(8,128)(2,1)}, u32[]{:S(2)}, u32[]{:S(2)}) collective-permute-start(bf16[3,2,3,32,1024]{4,3,2,0,1:T(8,128)(2,1)} %copy.33), channel_id=1, source_target_pairs={{0,2},{2,0},{1,3},{3,1},{4,6},{6,4},{5,7},{7,5},{8,10},{10,8},{9,1... | collective-permute-start | bytes 3538952 | tf_op jit(solution)/shard_map/ppermute | solution.py:71
  98.5 13.7 %all-to-all-done.1 = bf16[8,6,32,256]{3,2,1,0:T(8,128)(2,1)S(1)} async-done(((bf16[8,6,32,256]{3,2,1,0:T(8,128)(2,1)}), bf16[8,6,32,256]{3,2,1,0:T(8,128)(2,1)S(1)}, u32[]{:S(2)}, u32[]{:S(2)}) %all-to-all-start.1) | async-done | bytes 786464 | tf_op jit(solution)/shard_map/all_to_all | solution.py:56
  113.2 2.3 %collective-permute-start.1 = (bf16[6,32,2048]{2,1,0:T(8,128)(2,1)}, bf16[6,32,2048]{2,1,0:T(8,128)(2,1)}, u32[]{:S(2)}, u32[]{:S(2)}) collective-permute-start(bf16[6,32,2048]{2,1,0:T(8,128)(2,1)} %bitcast.41), channel_id=1, source_target_pairs={{0,2},{2,0},{1,3},{3,1},{4,6},{6,4},{5,7},{7,5},{8,10},{10,8},{9,1... | collective-permute-start | bytes 2359304 | tf_op jit(solution)/shard_map/ppermute | solution.py:72
  115.5 1.6 maximum_bitcast_fusion.2
  117.8 3.3 %fusion.113 = f32[192,1024]{1,0:T(8,128)S(1)} fusion(bf16[192,2048]{1,0:T(8,128)(2,1)S(1)} %bitcast.103, bf16[2048,1024]{1,0:T(8,128)(2,1)} %all-gather.2.cloned.1.call-done), kind=kOutput, calls=%fused_computation.246 | convolution fusion | flops 805306368 | bytes 5767168 | tf_op jit(solution)/shard_map/dot_general | solution.py:73
  121.2 2.3 %fusion.114 = f32[192,1024]{1,0:T(8,128)S(1)} fusion(bf16[192,2048]{1,0:T(8,128)(2,1)} %bitcast.21, bf16[2048,1024]{1,0:T(8,128)(2,1)S(1)} %copy-done.2), kind=kOutput, calls=%fused_computation.247 | convolution fusion | flops 805306368 | bytes 5767168 | tf_op jit(solution)/shard_map/dot_general | solution.py:73
  123.6 1.8 fusion.61
  126.3 1.9 collective-permute-start.7
  128.2 2.2 %collective-permute-start.3 = (f32[3,1,32,1024]{3,2,1,0:T(8,128)S(1)}, f32[3,1,32,1024]{3,2,1,0:T(8,128)S(1)}, u32[]{:S(2)}, u32[]{:S(2)}) collective-permute-start(f32[3,1,32,1024]{3,2,1,0:T(8,128)S(1)} %get-tuple-element.57), channel_id=1, source_target_pairs={{1,0},{3,2},{5,4},{7,6},{9,8},{11,10},{13,12},{15,14},{17,16},{19,... | collective-permute-start | bytes 1179656 | tf_op jit(solution)/shard_map/ppermute | solution.py:15
  130.4 1.3 collective-permute-start.2
  131.8 4.2 %collective-permute-start.5 = (f32[3,3,1,1024]{3,2,1,0:T(1,128)S(1)}, f32[3,3,1,1024]{3,2,1,0:T(1,128)S(1)}, u32[]{:S(2)}, u32[]{:S(2)}) collective-permute-start(f32[3,3,1,1024]{3,2,1,0:T(1,128)S(1)} %get-tuple-element.53), channel_id=1, source_target_pairs={{4,0},{8,4},{12,8},{16,12},{20,16},{24,20},{28,24},{5,1},{9,5},{13... | collective-permute-start | bytes 110600 | tf_op jit(solution)/shard_map/ppermute | solution.py:15
  136.0 1.9 collective-permute-start.4
  137.9 1.3 collective-permute-start.6
  139.4 1.8 collective-permute-done.6
  141.6 1.8 collective-permute-done.2
  143.4 1.6 fusion.17
  146.7 2.4 %collective-permute-start.13 = (f32[3,3,32,1]{3,2,1,0:T(8,128)S(1)}, f32[3,3,32,1]{3,2,1,0:T(8,128)S(1)}, u32[]{:S(2)}, u32[]{:S(2)}) collective-permute-start(f32[3,3,32,1]{3,2,1,0:T(8,128)S(1)} %get-tuple-element.31), channel_id=1, source_target_pairs={{2,0},{3,1},{6,4},{7,5},{10,8},{11,9},{14,12},{15,13},{18,16},{19,... | collective-permute-start | bytes 3464 | tf_op jit(solution)/shard_map/ppermute | solution.py:15
  149.1 3.1 %collective-permute-start.9 = (f32[3,1,32,1024]{3,2,1,0:T(8,128)S(1)}, f32[3,1,32,1024]{3,2,1,0:T(8,128)S(1)}, u32[]{:S(2)}, u32[]{:S(2)}) collective-permute-start(f32[3,1,32,1024]{3,2,1,0:T(8,128)S(1)} %get-tuple-element.39), channel_id=1, source_target_pairs={{1,0},{3,2},{5,4},{7,6},{9,8},{11,10},{13,12},{15,14},{17,16},{19,... | collective-permute-start | bytes 1179656 | tf_op jit(solution)/shard_map/ppermute | solution.py:15
  152.3 1.3 collective-permute-start.8
  154.1 2.7 %collective-permute-start.11 = (f32[3,3,1,1024]{3,2,1,0:T(1,128)S(1)}, f32[3,3,1,1024]{3,2,1,0:T(1,128)S(1)}, u32[]{:S(2)}, u32[]{:S(2)}) collective-permute-start(f32[3,3,1,1024]{3,2,1,0:T(1,128)S(1)} %get-tuple-element.35), channel_id=1, source_target_pairs={{4,0},{8,4},{12,8},{16,12},{20,16},{24,20},{28,24},{5,1},{9,5},{13... | collective-permute-start | bytes 110600 | tf_op jit(solution)/shard_map/ppermute | solution.py:15
  156.8 2.6 %collective-permute-start.10 = (f32[3,3,1,1024]{3,2,1,0:T(1,128)S(1)}, f32[3,3,1,1024]{3,2,1,0:T(1,128)S(1)}, u32[]{:S(2)}, u32[]{:S(2)}) collective-permute-start(f32[3,3,1,1024]{3,2,1,0:T(1,128)S(1)} %get-tuple-element.36), channel_id=1, source_target_pairs={{0,4},{4,8},{8,12},{12,16},{16,20},{20,24},{24,28},{1,5},{5,9},{9,... | collective-permute-start | bytes 110600 | tf_op jit(solution)/shard_map/ppermute | solution.py:14
  159.4 1.5 collective-permute-start.12
  161.1 1.6 collective-permute-done.12
  162.6 2.5 %collective-permute-done.8 = f32[3,1,32,1024]{3,2,1,0:T(8,128)S(1)} collective-permute-done((f32[3,1,32,1024]{3,2,1,0:T(8,128)S(1)}, f32[3,1,32,1024]{3,2,1,0:T(8,128)S(1)}, u32[]{:S(2)}, u32[]{:S(2)}) %collective-permute-start.8) | collective-permute-done | bytes 393248 | tf_op jit(solution)/shard_map/ppermute | solution.py:14
  165.2 1.6 fusion.29
  167.5 2.4 %collective-permute-start.19 = (f32[3,3,32,1]{3,2,1,0:T(8,128)S(1)}, f32[3,3,32,1]{3,2,1,0:T(8,128)S(1)}, u32[]{:S(2)}, u32[]{:S(2)}) collective-permute-start(f32[3,3,32,1]{3,2,1,0:T(8,128)S(1)} %get-tuple-element.19), channel_id=1, source_target_pairs={{2,0},{3,1},{6,4},{7,5},{10,8},{11,9},{14,12},{15,13},{18,16},{19,... | collective-permute-start | bytes 3464 | tf_op jit(solution)/shard_map/ppermute | solution.py:15
  169.9 2.1 collective-permute-start.15
  172.0 1.3 collective-permute-start.14
  173.8 2.7 %collective-permute-start.17 = (f32[3,3,1,1024]{3,2,1,0:T(1,128)S(1)}, f32[3,3,1,1024]{3,2,1,0:T(1,128)S(1)}, u32[]{:S(2)}, u32[]{:S(2)}) collective-permute-start(f32[3,3,1,1024]{3,2,1,0:T(1,128)S(1)} %get-tuple-element.23), channel_id=1, source_target_pairs={{4,0},{8,4},{12,8},{16,12},{20,16},{24,20},{28,24},{5,1},{9,5},{13... | collective-permute-start | bytes 110600 | tf_op jit(solution)/shard_map/ppermute | solution.py:15
  176.5 2.6 %collective-permute-start.16 = (f32[3,3,1,1024]{3,2,1,0:T(1,128)S(1)}, f32[3,3,1,1024]{3,2,1,0:T(1,128)S(1)}, u32[]{:S(2)}, u32[]{:S(2)}) collective-permute-start(f32[3,3,1,1024]{3,2,1,0:T(1,128)S(1)} %get-tuple-element.24), channel_id=1, source_target_pairs={{0,4},{4,8},{8,12},{12,16},{16,20},{20,24},{24,28},{1,5},{5,9},{9,... | collective-permute-start | bytes 110600 | tf_op jit(solution)/shard_map/ppermute | solution.py:14
  180.6 1.8 collective-permute-done.18
  182.4 2.5 %collective-permute-done.14 = f32[3,1,32,1024]{3,2,1,0:T(8,128)S(1)} collective-permute-done((f32[3,1,32,1024]{3,2,1,0:T(8,128)S(1)}, f32[3,1,32,1024]{3,2,1,0:T(8,128)S(1)}, u32[]{:S(2)}, u32[]{:S(2)}) %collective-permute-start.14) | collective-permute-done | bytes 393248 | tf_op jit(solution)/shard_map/ppermute | solution.py:14
  184.9 1.6 fusion.41
  187.2 2.4 %collective-permute-start.25 = (f32[3,3,32,1]{3,2,1,0:T(8,128)S(1)}, f32[3,3,32,1]{3,2,1,0:T(8,128)S(1)}, u32[]{:S(2)}, u32[]{:S(2)}) collective-permute-start(f32[3,3,32,1]{3,2,1,0:T(8,128)S(1)} %get-tuple-element.7), channel_id=1, source_target_pairs={{2,0},{3,1},{6,4},{7,5},{10,8},{11,9},{14,12},{15,13},{18,16},{19,... | collective-permute-start | bytes 3464 | tf_op jit(solution)/shard_map/ppermute | solution.py:15
  189.6 2.1 collective-permute-start.21
  191.7 1.3 collective-permute-start.20
  193.5 2.7 %collective-permute-start.23 = (f32[3,3,1,1024]{3,2,1,0:T(1,128)S(1)}, f32[3,3,1,1024]{3,2,1,0:T(1,128)S(1)}, u32[]{:S(2)}, u32[]{:S(2)}) collective-permute-start(f32[3,3,1,1024]{3,2,1,0:T(1,128)S(1)} %get-tuple-element.11), channel_id=1, source_target_pairs={{4,0},{8,4},{12,8},{16,12},{20,16},{24,20},{28,24},{5,1},{9,5},{13... | collective-permute-start | bytes 110600 | tf_op jit(solution)/shard_map/ppermute | solution.py:15
  196.2 2.6 %collective-permute-start.22 = (f32[3,3,1,1024]{3,2,1,0:T(1,128)S(1)}, f32[3,3,1,1024]{3,2,1,0:T(1,128)S(1)}, u32[]{:S(2)}, u32[]{:S(2)}) collective-permute-start(f32[3,3,1,1024]{3,2,1,0:T(1,128)S(1)} %get-tuple-element.12), channel_id=1, source_target_pairs={{0,4},{4,8},{8,12},{12,16},{16,20},{20,24},{24,28},{1,5},{5,9},{9,... | collective-permute-start | bytes 110600 | tf_op jit(solution)/shard_map/ppermute | solution.py:14
  200.3 1.8 collective-permute-done.24
  202.1 2.5 %collective-permute-done.20 = f32[3,1,32,1024]{3,2,1,0:T(8,128)S(1)} collective-permute-done((f32[3,1,32,1024]{3,2,1,0:T(8,128)S(1)}, f32[3,1,32,1024]{3,2,1,0:T(8,128)S(1)}, u32[]{:S(2)}, u32[]{:S(2)}) %collective-permute-start.20) | collective-permute-done | bytes 393248 | tf_op jit(solution)/shard_map/ppermute | solution.py:14
  204.6 1.6 fusion.53
  (90 shorter events, 21.4 us)
Async XLA Ops:
  6.5 1.2 copy-start
  6.5 2.1 copy-start.6
  6.5 111.2 %all-gather.2.cloned.1.call-start = ((), (), s32[]{:S(2)}) async-start(), calls=%async_computation.2 | async-start | bytes 4718592 | tf_op jit(solution)/shard_map/all_gather | solution.py:46
  18.6 5.8 %copy-start.7 = (bf16[32,256]{1,0:T(8,128)(2,1)S(1)}, bf16[32,256]{1,0:T(8,128)(2,1)}, u32[]{:S(2)}) copy-start(bf16[32,256]{1,0:T(8,128)(2,1)} %param.9) | copy-start | bytes 49156
  18.6 53.7 %all-to-all-start = ((bf16[8,2,24576]{2,1,0:T(2,128)(2,1)}), bf16[8,2,24576]{2,1,0:T(2,128)(2,1)S(1)}, u32[]{:S(2)}, u32[]{:S(2)}) async-start(bf16[8,2,24576]{2,1,0:T(2,128)(2,1)} %reshape.39), calls=%async_computation | async-start | bytes 1572864 | tf_op jit(solution)/shard_map/all_to_all | solution.py:52
  83.5 7.1 %copy-start.4 = (bf16[3,2,3,32,2048]{4,3,2,1,0:T(8,128)(2,1)S(1)}, bf16[3,2,3,32,2048]{4,3,2,1,0:T(8,128)(2,1)}, u32[]{:S(2)}) copy-start(bf16[3,2,3,32,2048]{4,3,2,1,0:T(8,128)(2,1)} %param.7) | copy-start | bytes 7077892
  86.0 26.2 %all-to-all-start.1 = ((bf16[8,6,32,256]{3,2,1,0:T(8,128)(2,1)}), bf16[8,6,32,256]{3,2,1,0:T(8,128)(2,1)S(1)}, u32[]{:S(2)}, u32[]{:S(2)}) async-start(bf16[8,6,32,256]{3,2,1,0:T(8,128)(2,1)} %fusion.91), calls=%async_computation.1 | async-start | bytes 1572864 | tf_op jit(solution)/shard_map/all_to_all | solution.py:56
  91.8 31.8 %collective-permute-start = (bf16[3,2,3,32,1024]{4,3,2,0,1:T(8,128)(2,1)}, bf16[3,2,3,32,1024]{4,3,2,0,1:T(8,128)(2,1)}, u32[]{:S(2)}, u32[]{:S(2)}) collective-permute-start(bf16[3,2,3,32,1024]{4,3,2,0,1:T(8,128)(2,1)} %copy.33), channel_id=1, source_target_pairs={{0,2},{2,0},{1,3},{3,1},{4,6},{6,4},{5,7},{7,5},{8,10},{10,8},{9,1... | collective-permute-start | bytes 3538952 | tf_op jit(solution)/shard_map/ppermute | solution.py:71
  113.2 8.0 %collective-permute-start.1 = (bf16[6,32,2048]{2,1,0:T(8,128)(2,1)}, bf16[6,32,2048]{2,1,0:T(8,128)(2,1)}, u32[]{:S(2)}, u32[]{:S(2)}) collective-permute-start(bf16[6,32,2048]{2,1,0:T(8,128)(2,1)} %bitcast.41), channel_id=1, source_target_pairs={{0,2},{2,0},{1,3},{3,1},{4,6},{6,4},{5,7},{7,5},{8,10},{10,8},{9,1... | collective-permute-start | bytes 2359304 | tf_op jit(solution)/shard_map/ppermute | solution.py:72
  117.7 3.5 %copy-start.2 = (bf16[2048,1024]{1,0:T(8,128)(2,1)S(1)}, bf16[2048,1024]{1,0:T(8,128)(2,1)}, u32[]{:S(2)}) copy-start(bf16[2048,1024]{1,0:T(8,128)(2,1)} %all-gather.2.cloned.1.call-done) | copy-start | bytes 12582916
  121.2 2.4 %copy-start.5 = (bf16[3,2,3,32,2048]{4,3,2,1,0:T(8,128)(2,1)S(1)}, bf16[3,2,3,32,2048]{4,3,2,1,0:T(8,128)(2,1)}, u32[]{:S(2)}) copy-start(bf16[3,2,3,32,2048]{4,3,2,1,0:T(8,128)(2,1)} %param.7) | copy-start | bytes 7077892
  126.3 11.6 %collective-permute-start.7 = (f32[3,3,32,1]{3,2,1,0:T(8,128)S(1)}, f32[3,3,32,1]{3,2,1,0:T(8,128)S(1)}, u32[]{:S(2)}, u32[]{:S(2)}) collective-permute-start(f32[3,3,32,1]{3,2,1,0:T(8,128)S(1)} %get-tuple-element.49), channel_id=1, source_target_pairs={{2,0},{3,1},{6,4},{7,5},{10,8},{11,9},{14,12},{15,13},{18,16},{19,... | collective-permute-start | bytes 3464 | tf_op jit(solution)/shard_map/ppermute | solution.py:15
  128.2 13.4 %collective-permute-start.3 = (f32[3,1,32,1024]{3,2,1,0:T(8,128)S(1)}, f32[3,1,32,1024]{3,2,1,0:T(8,128)S(1)}, u32[]{:S(2)}, u32[]{:S(2)}) collective-permute-start(f32[3,1,32,1024]{3,2,1,0:T(8,128)S(1)} %get-tuple-element.57), channel_id=1, source_target_pairs={{1,0},{3,2},{5,4},{7,6},{9,8},{11,10},{13,12},{15,14},{17,16},{19,... | collective-permute-start | bytes 1179656 | tf_op jit(solution)/shard_map/ppermute | solution.py:15
  130.4 12.9 %collective-permute-start.2 = (f32[3,1,32,1024]{3,2,1,0:T(8,128)S(1)}, f32[3,1,32,1024]{3,2,1,0:T(8,128)S(1)}, u32[]{:S(2)}, u32[]{:S(2)}) collective-permute-start(f32[3,1,32,1024]{3,2,1,0:T(8,128)S(1)} %get-tuple-element.58), channel_id=1, source_target_pairs={{0,1},{2,3},{4,5},{6,7},{8,9},{10,11},{12,13},{14,15},{16,17},{18,... | collective-permute-start | bytes 1179656 | tf_op jit(solution)/shard_map/ppermute | solution.py:14
  131.8 9.4 %collective-permute-start.5 = (f32[3,3,1,1024]{3,2,1,0:T(1,128)S(1)}, f32[3,3,1,1024]{3,2,1,0:T(1,128)S(1)}, u32[]{:S(2)}, u32[]{:S(2)}) collective-permute-start(f32[3,3,1,1024]{3,2,1,0:T(1,128)S(1)} %get-tuple-element.53), channel_id=1, source_target_pairs={{4,0},{8,4},{12,8},{16,12},{20,16},{24,20},{28,24},{5,1},{9,5},{13... | collective-permute-start | bytes 110600 | tf_op jit(solution)/shard_map/ppermute | solution.py:15
  136.0 5.6 %collective-permute-start.4 = (f32[3,3,1,1024]{3,2,1,0:T(1,128)S(1)}, f32[3,3,1,1024]{3,2,1,0:T(1,128)S(1)}, u32[]{:S(2)}, u32[]{:S(2)}) collective-permute-start(f32[3,3,1,1024]{3,2,1,0:T(1,128)S(1)} %get-tuple-element.54), channel_id=1, source_target_pairs={{0,4},{4,8},{8,12},{12,16},{16,20},{20,24},{24,28},{1,5},{5,9},{9,... | collective-permute-start | bytes 110600 | tf_op jit(solution)/shard_map/ppermute | solution.py:14
  137.9 3.3 %collective-permute-start.6 = (f32[3,3,32,1]{3,2,1,0:T(8,128)S(1)}, f32[3,3,32,1]{3,2,1,0:T(8,128)S(1)}, u32[]{:S(2)}, u32[]{:S(2)}) collective-permute-start(f32[3,3,32,1]{3,2,1,0:T(8,128)S(1)} %get-tuple-element.50), channel_id=1, source_target_pairs={{0,2},{1,3},{4,6},{5,7},{8,10},{9,11},{12,14},{13,15},{16,18},{17,... | collective-permute-start | bytes 3464 | tf_op jit(solution)/shard_map/ppermute | solution.py:14
  145.0 1.1 copy-start.3
  146.7 12.7 %collective-permute-start.13 = (f32[3,3,32,1]{3,2,1,0:T(8,128)S(1)}, f32[3,3,32,1]{3,2,1,0:T(8,128)S(1)}, u32[]{:S(2)}, u32[]{:S(2)}) collective-permute-start(f32[3,3,32,1]{3,2,1,0:T(8,128)S(1)} %get-tuple-element.31), channel_id=1, source_target_pairs={{2,0},{3,1},{6,4},{7,5},{10,8},{11,9},{14,12},{15,13},{18,16},{19,... | collective-permute-start | bytes 3464 | tf_op jit(solution)/shard_map/ppermute | solution.py:15
  149.1 13.5 %collective-permute-start.9 = (f32[3,1,32,1024]{3,2,1,0:T(8,128)S(1)}, f32[3,1,32,1024]{3,2,1,0:T(8,128)S(1)}, u32[]{:S(2)}, u32[]{:S(2)}) collective-permute-start(f32[3,1,32,1024]{3,2,1,0:T(8,128)S(1)} %get-tuple-element.39), channel_id=1, source_target_pairs={{1,0},{3,2},{5,4},{7,6},{9,8},{11,10},{13,12},{15,14},{17,16},{19,... | collective-permute-start | bytes 1179656 | tf_op jit(solution)/shard_map/ppermute | solution.py:15
  152.3 12.9 %collective-permute-start.8 = (f32[3,1,32,1024]{3,2,1,0:T(8,128)S(1)}, f32[3,1,32,1024]{3,2,1,0:T(8,128)S(1)}, u32[]{:S(2)}, u32[]{:S(2)}) collective-permute-start(f32[3,1,32,1024]{3,2,1,0:T(8,128)S(1)} %get-tuple-element.40), channel_id=1, source_target_pairs={{0,1},{2,3},{4,5},{6,7},{8,9},{10,11},{12,13},{14,15},{16,17},{18,... | collective-permute-start | bytes 1179656 | tf_op jit(solution)/shard_map/ppermute | solution.py:14
  154.1 8.6 %collective-permute-start.11 = (f32[3,3,1,1024]{3,2,1,0:T(1,128)S(1)}, f32[3,3,1,1024]{3,2,1,0:T(1,128)S(1)}, u32[]{:S(2)}, u32[]{:S(2)}) collective-permute-start(f32[3,3,1,1024]{3,2,1,0:T(1,128)S(1)} %get-tuple-element.35), channel_id=1, source_target_pairs={{4,0},{8,4},{12,8},{16,12},{20,16},{24,20},{28,24},{5,1},{9,5},{13... | collective-permute-start | bytes 110600 | tf_op jit(solution)/shard_map/ppermute | solution.py:15
  156.8 5.9 %collective-permute-start.10 = (f32[3,3,1,1024]{3,2,1,0:T(1,128)S(1)}, f32[3,3,1,1024]{3,2,1,0:T(1,128)S(1)}, u32[]{:S(2)}, u32[]{:S(2)}) collective-permute-start(f32[3,3,1,1024]{3,2,1,0:T(1,128)S(1)} %get-tuple-element.36), channel_id=1, source_target_pairs={{0,4},{4,8},{8,12},{12,16},{16,20},{20,24},{24,28},{1,5},{5,9},{9,... | collective-permute-start | bytes 110600 | tf_op jit(solution)/shard_map/ppermute | solution.py:14
  159.4 3.3 %collective-permute-start.12 = (f32[3,3,32,1]{3,2,1,0:T(8,128)S(1)}, f32[3,3,32,1]{3,2,1,0:T(8,128)S(1)}, u32[]{:S(2)}, u32[]{:S(2)}) collective-permute-start(f32[3,3,32,1]{3,2,1,0:T(8,128)S(1)} %get-tuple-element.32), channel_id=1, source_target_pairs={{0,2},{1,3},{4,6},{5,7},{8,10},{9,11},{12,14},{13,15},{16,18},{17,... | collective-permute-start | bytes 3464 | tf_op jit(solution)/shard_map/ppermute | solution.py:14
  167.5 11.6 %collective-permute-start.19 = (f32[3,3,32,1]{3,2,1,0:T(8,128)S(1)}, f32[3,3,32,1]{3,2,1,0:T(8,128)S(1)}, u32[]{:S(2)}, u32[]{:S(2)}) collective-permute-start(f32[3,3,32,1]{3,2,1,0:T(8,128)S(1)} %get-tuple-element.19), channel_id=1, source_target_pairs={{2,0},{3,1},{6,4},{7,5},{10,8},{11,9},{14,12},{15,13},{18,16},{19,... | collective-permute-start | bytes 3464 | tf_op jit(solution)/shard_map/ppermute | solution.py:15
  169.9 12.5 %collective-permute-start.15 = (f32[3,1,32,1024]{3,2,1,0:T(8,128)S(1)}, f32[3,1,32,1024]{3,2,1,0:T(8,128)S(1)}, u32[]{:S(2)}, u32[]{:S(2)}) collective-permute-start(f32[3,1,32,1024]{3,2,1,0:T(8,128)S(1)} %get-tuple-element.27), channel_id=1, source_target_pairs={{1,0},{3,2},{5,4},{7,6},{9,8},{11,10},{13,12},{15,14},{17,16},{19,... | collective-permute-start | bytes 1179656 | tf_op jit(solution)/shard_map/ppermute | solution.py:15
  172.0 12.9 %collective-permute-start.14 = (f32[3,1,32,1024]{3,2,1,0:T(8,128)S(1)}, f32[3,1,32,1024]{3,2,1,0:T(8,128)S(1)}, u32[]{:S(2)}, u32[]{:S(2)}) collective-permute-start(f32[3,1,32,1024]{3,2,1,0:T(8,128)S(1)} %get-tuple-element.28), channel_id=1, source_target_pairs={{0,1},{2,3},{4,5},{6,7},{8,9},{10,11},{12,13},{14,15},{16,17},{18,... | collective-permute-start | bytes 1179656 | tf_op jit(solution)/shard_map/ppermute | solution.py:14
  173.8 8.6 %collective-permute-start.17 = (f32[3,3,1,1024]{3,2,1,0:T(1,128)S(1)}, f32[3,3,1,1024]{3,2,1,0:T(1,128)S(1)}, u32[]{:S(2)}, u32[]{:S(2)}) collective-permute-start(f32[3,3,1,1024]{3,2,1,0:T(1,128)S(1)} %get-tuple-element.23), channel_id=1, source_target_pairs={{4,0},{8,4},{12,8},{16,12},{20,16},{24,20},{28,24},{5,1},{9,5},{13... | collective-permute-start | bytes 110600 | tf_op jit(solution)/shard_map/ppermute | solution.py:15
  176.5 5.9 %collective-permute-start.16 = (f32[3,3,1,1024]{3,2,1,0:T(1,128)S(1)}, f32[3,3,1,1024]{3,2,1,0:T(1,128)S(1)}, u32[]{:S(2)}, u32[]{:S(2)}) collective-permute-start(f32[3,3,1,1024]{3,2,1,0:T(1,128)S(1)} %get-tuple-element.24), channel_id=1, source_target_pairs={{0,4},{4,8},{8,12},{12,16},{16,20},{20,24},{24,28},{1,5},{5,9},{9,... | collective-permute-start | bytes 110600 | tf_op jit(solution)/shard_map/ppermute | solution.py:14
  179.1 3.3 %collective-permute-start.18 = (f32[3,3,32,1]{3,2,1,0:T(8,128)S(1)}, f32[3,3,32,1]{3,2,1,0:T(8,128)S(1)}, u32[]{:S(2)}, u32[]{:S(2)}) collective-permute-start(f32[3,3,32,1]{3,2,1,0:T(8,128)S(1)} %get-tuple-element.20), channel_id=1, source_target_pairs={{0,2},{1,3},{4,6},{5,7},{8,10},{9,11},{12,14},{13,15},{16,18},{17,... | collective-permute-start | bytes 3464 | tf_op jit(solution)/shard_map/ppermute | solution.py:14
  187.2 11.6 %collective-permute-start.25 = (f32[3,3,32,1]{3,2,1,0:T(8,128)S(1)}, f32[3,3,32,1]{3,2,1,0:T(8,128)S(1)}, u32[]{:S(2)}, u32[]{:S(2)}) collective-permute-start(f32[3,3,32,1]{3,2,1,0:T(8,128)S(1)} %get-tuple-element.7), channel_id=1, source_target_pairs={{2,0},{3,1},{6,4},{7,5},{10,8},{11,9},{14,12},{15,13},{18,16},{19,... | collective-permute-start | bytes 3464 | tf_op jit(solution)/shard_map/ppermute | solution.py:15
  189.6 12.5 %collective-permute-start.21 = (f32[3,1,32,1024]{3,2,1,0:T(8,128)S(1)}, f32[3,1,32,1024]{3,2,1,0:T(8,128)S(1)}, u32[]{:S(2)}, u32[]{:S(2)}) collective-permute-start(f32[3,1,32,1024]{3,2,1,0:T(8,128)S(1)} %get-tuple-element.15), channel_id=1, source_target_pairs={{1,0},{3,2},{5,4},{7,6},{9,8},{11,10},{13,12},{15,14},{17,16},{19,... | collective-permute-start | bytes 1179656 | tf_op jit(solution)/shard_map/ppermute | solution.py:15
  191.7 12.9 %collective-permute-start.20 = (f32[3,1,32,1024]{3,2,1,0:T(8,128)S(1)}, f32[3,1,32,1024]{3,2,1,0:T(8,128)S(1)}, u32[]{:S(2)}, u32[]{:S(2)}) collective-permute-start(f32[3,1,32,1024]{3,2,1,0:T(8,128)S(1)} %get-tuple-element.16), channel_id=1, source_target_pairs={{0,1},{2,3},{4,5},{6,7},{8,9},{10,11},{12,13},{14,15},{16,17},{18,... | collective-permute-start | bytes 1179656 | tf_op jit(solution)/shard_map/ppermute | solution.py:14
  193.5 8.6 %collective-permute-start.23 = (f32[3,3,1,1024]{3,2,1,0:T(1,128)S(1)}, f32[3,3,1,1024]{3,2,1,0:T(1,128)S(1)}, u32[]{:S(2)}, u32[]{:S(2)}) collective-permute-start(f32[3,3,1,1024]{3,2,1,0:T(1,128)S(1)} %get-tuple-element.11), channel_id=1, source_target_pairs={{4,0},{8,4},{12,8},{16,12},{20,16},{24,20},{28,24},{5,1},{9,5},{13... | collective-permute-start | bytes 110600 | tf_op jit(solution)/shard_map/ppermute | solution.py:15
  196.2 5.9 %collective-permute-start.22 = (f32[3,3,1,1024]{3,2,1,0:T(1,128)S(1)}, f32[3,3,1,1024]{3,2,1,0:T(1,128)S(1)}, u32[]{:S(2)}, u32[]{:S(2)}) collective-permute-start(f32[3,3,1,1024]{3,2,1,0:T(1,128)S(1)} %get-tuple-element.12), channel_id=1, source_target_pairs={{0,4},{4,8},{8,12},{12,16},{16,20},{20,24},{24,28},{1,5},{5,9},{9,... | collective-permute-start | bytes 110600 | tf_op jit(solution)/shard_map/ppermute | solution.py:14
  198.8 3.3 %collective-permute-start.24 = (f32[3,3,32,1]{3,2,1,0:T(8,128)S(1)}, f32[3,3,32,1]{3,2,1,0:T(8,128)S(1)}, u32[]{:S(2)}, u32[]{:S(2)}) collective-permute-start(f32[3,3,32,1]{3,2,1,0:T(8,128)S(1)} %get-tuple-element.8), channel_id=1, source_target_pairs={{0,2},{1,3},{4,6},{5,7},{8,10},{9,11},{12,14},{13,15},{16,18},{17,... | collective-permute-start | bytes 3464 | tf_op jit(solution)/shard_map/ppermute | solution.py:14
  206.3 1.4 copy-start.1
Sparse Core Ops, SparseCore 0:
  9.5 89.8 all-gather.1
